TPU v7x, 32 devices: a whole 2x2x4 slice. The times are simulated.
32 devices in a mesh: scan: 2 (over y), ang: 4 (over z), row: 4 (over x, core).
Axes of the slice: x: 2, y: 2, z: 4, core: 2. Of those that a mesh axis runs over, the one named last changes fastest.
Arguments:
- projections: bfloat16 [8, 32, 2560], P(('scan', 'ang'), 'row'), parts along dimension 0, may hold values from 0 to 2
- flats: float32 [64, 2560], P(('scan', 'row')), parts along dimension 0, may hold values from 1 to 3
- block_start: int32 [4, 4], replicated, may hold values from 0 to 2528
- bp_weights: bfloat16 [4, 32, 1024], P(None, None, 'ang'), may hold values from -0.5 to 0.5
Outputs:
- recon: float32 [64, 1024], P(('scan', 'row'), 'ang'), parts along dimension 0
There are 2 independent parts, one for each index of `scan`. A program takes and returns all parts, laid end to end along the dimension named above; an argument that names none is the same for every part. Nothing has to cross between parts.
Inputs may be any that keep to these rules, and one draw needn't show every extreme that they name: block_start[a, r] is the first of the 32 detector columns that pixel region r reads at angle a.
All inputs are finite; a program needn't handle non-finite values.
Results may differ from a plain program's by a relative error of at most 0.009.
Values may be sent and summed in bfloat16 or wider, within the bound.
A program may use at most 64 MiB of HBM per device.

v0:
```python
import functools

import jax
import jax.numpy as jnp
import numpy as np
from jax import lax
from jax.experimental import pallas as pl
from jax.experimental.pallas import tpu as pltpu
from jax.sharding import PartitionSpec as P

HALO = 4
LANES = 128
SHIFTS = 2
paganin_beta = 8.0
ramp_gain = 320.0


def filter_table(tile_rows, width, cb_width):
    u = np.arange(tile_rows, dtype=np.float64)
    v = np.arange(width, dtype=np.float64)
    lam = (4.0 * np.sin(np.pi * u / tile_rows) ** 2)[:, None] + (4.0 * np.sin(np.pi * v / width) ** 2)[None, :]
    folded = np.minimum(v, width - v)
    ramp = ramp_gain * (folded / width) * (0.5 + 0.5 * np.cos(2.0 * np.pi * folded / width))
    taps = np.real(np.fft.ifft2(ramp[None, :] / (1.0 + paganin_beta * lam)))
    lags = tile_rows // 2 + 1
    cb_width = cb_width // SHIFTS
    place = (np.arange(cb_width)[:, None] - np.arange(width)[None, :]) % width
    return taps[:lags][:, place].reshape(lags * cb_width, width)


def kernel(regions, tiles, starts, proj, flats, table, weights, out,
           starts_s, proj_v, flats_v, table_v, weights_v, xs, ys, sbuf, rbuf,
           load_sem, table_sem, send_sem, recv_sem):
    rows, width = flats.shape
    blocks = width // LANES
    angles, cb, _ = weights.shape
    per = LANES // cb
    half = rows // 2
    me = lax.axis_index("ang")
    row = lax.axis_index("row")

    def peer(step, delta):
        return {"ang": lax.rem(me + step, regions), "row": lax.rem(row + delta + tiles, tiles)}

    links = [(step, delta) for step in range(regions) for delta in (-1, 0, 1) if (step, delta) != (0, 0)]

    def when_there(delta, action):
        if delta == 0:
            action()
        else:
            pl.when(row > 0 if delta < 0 else row < tiles - 1)(action)

    loads = [pltpu.make_async_copy(proj.at[0], proj_v, load_sem.at[0]),
             pltpu.make_async_copy(flats, flats_v, load_sem.at[1]),
             pltpu.make_async_copy(starts, starts_s, load_sem.at[3])]
    late = [pltpu.make_async_copy(table, table_v, table_sem)]
    weight_load = pltpu.make_async_copy(weights, weights_v, load_sem.at[2])
    for copy in loads + late + [weight_load]:
        copy.start()

    barrier = pltpu.get_barrier_semaphore()
    for step, delta in links:
        when_there(delta, lambda: pl.semaphore_signal(
            barrier, inc=1, device_id=peer(step, delta), device_id_type=pl.DeviceIdType.MESH))
    zeros = jnp.zeros((angles, rows, LANES), jnp.bfloat16)
    pl.when(row == tiles - 1)(lambda: rbuf.at[0].__setitem__(..., zeros))
    pl.when(row == 0)(lambda: rbuf.at[2].__setitem__(..., zeros))

    for copy in loads:
        copy.wait()

    pieces = [slice(b * LANES, (b + 1) * LANES) for b in range(blocks)]
    contrast = [1.0 - proj_v[:, p].astype(jnp.float32) / flats_v[:, p] for p in pieces]
    mean = jnp.sum(sum(contrast), axis=1, keepdims=True) / width
    for b, x in enumerate(contrast):
        xs[b] = x - mean
        xs[b + blocks] = x - mean

    lane = lax.broadcasted_iota(jnp.int32, (rows, LANES), 1)
    sub = lax.broadcasted_iota(jnp.int32, (rows, LANES), 0)
    cs = cb // SHIFTS
    for g in range(regions):
        shifted = []
        for k in range(SHIFTS):
            start = starts_s[me, g] + k * cs
            first = start // LANES
            rest = lax.rem(start, LANES)
            shift = lax.rem(LANES - rest, LANES)
            low = lane < LANES - rest
            turned = [pltpu.roll(xs[first + b], shift, 1) for b in range(blocks + 1)]
            shifted.append([jnp.where(low, turned[b], turned[b + 1]) for b in range(blocks)])
        for b in range(blocks):
            ys[g * SHIFTS * rows:(g + 1) * SHIFTS * rows, b * LANES:(b + 1) * LANES] = jnp.concatenate(
                [y[b] for y in shifted], axis=0).astype(jnp.bfloat16)

    late[0].wait()
    total = lax.dot_general(ys[...], table_v[...], (((1,), (1,)), ((), ())), preferred_element_type=jnp.float32)

    lags = rows + 1
    pad = -(lags * cs) % LANES
    total = jnp.concatenate([total, jnp.zeros((total.shape[0], pad), jnp.float32)], axis=1)
    spot = lax.rem(me, per) * cb
    mine = (lane >= spot) & (lane < spot + cb)
    for g in range(regions):
        lag = []
        for d in range(lags):
            column = d * cs // LANES * LANES
            merged = None
            for k in range(SHIFTS):
                base = (g * SHIFTS + k) * rows
                tile = total[base:base + rows, column:column + LANES]
                tile = pltpu.roll(tile, lax.rem(spot + k * cs + LANES - d * cs % LANES, LANES), 1)
                merged = tile if k == 0 else jnp.where(lane < spot + k * cs, merged, tile)
            lag.append(merged)
        own = lag[0]
        after = jnp.where(sub >= half, lag[rows], 0.0)
        before = jnp.where(sub < half, lag[rows], 0.0)
        for e in range(1, rows):
            a = pltpu.roll(lag[e], e, 0)
            b = pltpu.roll(lag[rows - e], e, 0)
            own = own + jnp.where(sub >= e, a, b)
            other = jnp.where(sub >= e, b, a)
            source = lax.rem(sub + rows - e, rows)
            after = after + jnp.where(source >= half, other, 0.0)
            before = before + jnp.where(source < half, other, 0.0)
        sbuf[0, g] = jnp.where(mine, before, 0.0).astype(jnp.bfloat16)
        sbuf[1, g] = jnp.where(mine, own, 0.0).astype(jnp.bfloat16)
        sbuf[2, g] = jnp.where(mine, after, 0.0).astype(jnp.bfloat16)

    sides = (row > 0).astype(jnp.int32) + (row < tiles - 1).astype(jnp.int32)
    pl.semaphore_wait(barrier, regions - 1 + sides * regions)

    def message(step, delta):
        to = peer(step, delta)
        region = to["ang"]
        return pltpu.make_async_remote_copy(
            src_ref=sbuf.at[delta + 1, region], dst_ref=rbuf.at[delta + 1, me],
            send_sem=send_sem.at[delta + 1, region], recv_sem=recv_sem.at[delta + 1, me],
            device_id=to, device_id_type=pl.DeviceIdType.MESH)

    sent = [message(step, delta) for step, delta in links]
    for (step, delta), copy in zip(links, sent):
        when_there(delta, copy.start)
    weight_load.wait()

    def arrived(step, delta):
        angle = lax.rem(me + step, regions)
        copy = pltpu.make_async_remote_copy(
            src_ref=sbuf.at[delta + 1, angle], dst_ref=rbuf.at[delta + 1, angle],
            send_sem=send_sem.at[delta + 1, angle], recv_sem=recv_sem.at[delta + 1, angle],
            device_id=peer(step, delta), device_id_type=pl.DeviceIdType.MESH)
        when_there(-delta, copy.wait_recv)

    rbuf[1, me] = sbuf[1, me]
    for step, delta in links:
        arrived(step, delta)

    result = jnp.zeros(out.shape, jnp.float32)
    for group in range(-(-angles // per)):
        block = jnp.zeros((rows, LANES), jnp.float32)
        members = range(group * per, min(angles, (group + 1) * per))
        for a in members:
            block = block + rbuf[1, a].astype(jnp.float32)
            block = block + rbuf[0, a].astype(jnp.float32)
            block = block + rbuf[2, a].astype(jnp.float32)
        block = block.astype(jnp.bfloat16)
        depth = len(members) * cb
        w = weights_v[group * per:group * per + len(members)].reshape(depth, out.shape[1])
        result = result + jnp.dot(block[:, :depth], w, preferred_element_type=jnp.float32)
    out[...] = result
    for (step, delta), copy in zip(links, sent):
        when_there(delta, copy.wait_send)


def body(projections, flats, block_start, bp_weights):
    _, rows, width = projections.shape
    angles, cb, pixels = bp_weights.shape
    regions, tiles = lax.axis_size("ang"), lax.axis_size("row")
    table = jnp.asarray(filter_table(rows + 2 * HALO, width, cb), jnp.bfloat16)
    hbm = pl.BlockSpec(memory_space=pltpu.HBM)
    return pl.pallas_call(
        functools.partial(kernel, regions, tiles),
        name="fbp",
        out_shape=pltpu.VMEM((rows, pixels), jnp.float32),
        in_specs=[hbm, hbm, hbm, hbm, hbm],
        out_specs=pl.BlockSpec(memory_space=pltpu.VMEM),
        scratch_shapes=[
            pltpu.SMEM(block_start.shape, jnp.int32),
            pltpu.VMEM((rows, width), jnp.bfloat16),
            pltpu.VMEM((rows, width), jnp.float32),
            pltpu.VMEM(table.shape, jnp.bfloat16),
            pltpu.VMEM(bp_weights.shape, jnp.bfloat16),
            pltpu.VMEM((2 * width // LANES, rows, LANES), jnp.float32),
            pltpu.VMEM((regions * SHIFTS * rows, width), jnp.bfloat16),
            pltpu.VMEM((3, regions, rows, LANES), jnp.bfloat16),
            pltpu.VMEM((3, angles, rows, LANES), jnp.bfloat16),
            pltpu.SemaphoreType.DMA((4,)),
            pltpu.SemaphoreType.DMA,
            pltpu.SemaphoreType.DMA((3, regions)),
            pltpu.SemaphoreType.DMA((3, angles)),
        ],
        compiler_params=pltpu.CompilerParams(collective_id=0, has_side_effects=True, vmem_limit_bytes=65000000),
    )(block_start, projections, flats, table, bp_weights)


def solution(mesh):
    placed = (P(("scan", "ang"), "row", None), P(("scan", "row"), None), P(), P(None, None, "ang"))
    return jax.shard_map(
        body, mesh=mesh, in_specs=placed, out_specs=P(("scan", "row"), "ang"), check_vma=False
    )
```

profile of v0, /device:TPU:1, one launch (start us, length us, event | category | flops | bytes accessed | tf_op | source)
XLA Modules:
  0.0 9.6 jit_solution(5316032810069169426)
XLA Ops:
  0.0 9.0 %fbp.1 = f32[8,256]{1,0:T(8,128)S(1)} custom-call(s32[4,4]{1,0:T(4,128)} %starts.1, bf16[1,8,2560]{2,1,0:T(8,128)(2,1)} %proj.1, f32[8,2560]{1,0:T(8,128)} %flats.1, bf16[144,2560]{1,0:T(8,128)(2,1)} %constant.2.clone.table, bf16[4,32,256]{2,1,0:T(8,128)(2,1)} %weights.1), custom_call_target="tpu_custom_call" | custom-call | tf_op jit(solution)/shard_map/fbp/pallas_call | solution.py:181
  9.0 0.6 %copy.7 = f32[8,256]{1,0:T(8,128)} copy(f32[8,256]{1,0:T(8,128)S(1)} %fbp.1) | data formatting | bytes 16384
where the time goes:
time: 9.79 us; the launch traced here: 9.64 us
  Pallas kernels  9.03 us (92%)
  local copies, waits for them, and re-layouts  0.6 us (6%)
    pallas_call x1, Pallas kernels, body(): pl.pallas_call(functools.partial(kernel, regions, tiles), name='fbp', out...  9.03 us
    unnamed x1, local copies, waits for them, and re-layouts  0.6 us

commit v1 on v0

v1 whole, which is shorter than its diff:
```python
import functools

import jax
import jax.numpy as jnp
import numpy as np
from jax import lax
from jax.experimental import pallas as pl
from jax.experimental.pallas import tpu as pltpu
from jax.sharding import PartitionSpec as P

HALO = 4
LANES = 128
paganin_beta = 8.0
ramp_gain = 320.0


def filter_table(tile_rows, width, columns):
    u = np.arange(tile_rows, dtype=np.float64)
    v = np.arange(width, dtype=np.float64)
    lam = (4.0 * np.sin(np.pi * u / tile_rows) ** 2)[:, None] + (4.0 * np.sin(np.pi * v / width) ** 2)[None, :]
    folded = np.minimum(v, width - v)
    ramp = ramp_gain * (folded / width) * (0.5 + 0.5 * np.cos(2.0 * np.pi * folded / width))
    taps = np.real(np.fft.ifft2(ramp[None, :] / (1.0 + paganin_beta * lam)))
    lags = tile_rows // 2 + 1
    place = (np.arange(columns)[:, None] - np.arange(width)[None, :]) % width
    return taps[:lags][:, place].reshape(lags * columns, width)


def kernel(regions, tiles, starts, proj, flats, table, weights, out,
           starts_s, proj_v, flats_v, table_v, weights_v, xs, ys, sbuf, rbuf,
           load_sem, send_sem, recv_sem):
    rows, width = flats.shape
    blocks = width // LANES
    angles, cb, _ = weights.shape
    half = rows // 2
    cs = LANES // rows
    shifts = cb // cs
    me = lax.axis_index("ang")
    row = lax.axis_index("row")

    def peer(step, delta):
        return {"ang": lax.rem(me + step, regions), "row": lax.rem(row + delta + tiles, tiles)}

    links = [(step, delta) for step in (*range(1, regions), 0) for delta in (-1, 1, 0) if (step, delta) != (0, 0)]

    def when_there(delta, action):
        if delta == 0:
            action()
        else:
            pl.when(row > 0 if delta < 0 else row < tiles - 1)(action)

    loads = [pltpu.make_async_copy(proj.at[0], proj_v, load_sem.at[0]),
             pltpu.make_async_copy(flats, flats_v, load_sem.at[1]),
             pltpu.make_async_copy(starts, starts_s, load_sem.at[3])]
    table_load = pltpu.make_async_copy(table, table_v, load_sem.at[4])
    weight_load = pltpu.make_async_copy(weights, weights_v, load_sem.at[2])
    for copy in [*loads, table_load, weight_load]:
        copy.start()

    barrier = pltpu.get_barrier_semaphore()
    for step, delta in links:
        when_there(delta, lambda: pl.semaphore_signal(
            barrier, inc=1, device_id=peer(step, delta), device_id_type=pl.DeviceIdType.MESH))

    def slot(delta):
        return pl.ds((1 + delta) * rows, rows)

    zeros = jnp.zeros((angles, rows, shifts * LANES), jnp.bfloat16)
    pl.when(row == tiles - 1)(lambda: rbuf.at[:, slot(-1)].__setitem__(..., zeros))
    pl.when(row == 0)(lambda: rbuf.at[:, slot(1)].__setitem__(..., zeros))

    lane = lax.broadcasted_iota(jnp.int32, (rows, LANES), 1)
    sub = lax.broadcasted_iota(jnp.int32, (rows, LANES), 0)

    for copy in loads:
        copy.wait()

    pieces = [slice(b * LANES, (b + 1) * LANES) for b in range(blocks)]
    contrast = [1.0 - proj_v[:, p].astype(jnp.float32) / flats_v[:, p] for p in pieces]
    mean = jnp.sum(sum(contrast), axis=1, keepdims=True) / width
    for b, x in enumerate(contrast):
        xs[b] = x - mean
        xs[b + blocks] = x - mean

    for g in range(regions):
        shifted = []
        for k in range(shifts):
            start = starts_s[me, g] + k * cs
            first = start // LANES
            rest = lax.rem(start, LANES)
            shift = lax.rem(LANES - rest, LANES)
            low = lane < LANES - rest
            turned = [pltpu.roll(xs[first + b], shift, 1) for b in range(blocks + 1)]
            shifted.append([jnp.where(low, turned[b], turned[b + 1]) for b in range(blocks)])
        for b in range(blocks):
            ys[g * shifts * rows:(g + 1) * shifts * rows, b * LANES:(b + 1) * LANES] = jnp.concatenate(
                [y[b] for y in shifted], axis=0).astype(jnp.bfloat16)

    table_load.wait()
    total = lax.dot_general(ys[...], table_v[...], (((1,), (1,)), ((), ())), preferred_element_type=jnp.float32)
    total = jnp.concatenate([total, jnp.zeros((total.shape[0], LANES - cs), jnp.float32)], axis=1)

    lag = lane // cs
    up, down = lax.rem(sub + rows - lag, rows), lax.rem(sub + lag, rows)
    inside = [sub >= lag, (lag > 0) & (sub + lag < rows)]
    wrapped = [(sub < lag) | (lag == 0), sub + lag >= rows]
    parts = {0: inside,
             -1: [wrapped[0] & (up < half), wrapped[1] & (down < half)],
             1: [wrapped[0] & (up >= half), wrapped[1] & (down >= half)]}
    bits = [1 << n for n in range((rows - 1).bit_length())]
    for g in range(regions):
        for k in range(shifts):
            base = (g * shifts + k) * rows
            tile = total[base:base + rows, :LANES]
            last = total[base:base + rows, LANES:]
            ahead, back = tile, tile
            for bit in bits:
                turn = (lag & bit) > 0
                ahead = jnp.where(turn, pltpu.roll(ahead, bit, 0), ahead)
                back = jnp.where(turn, pltpu.roll(back, rows - bit, 0), back)
            edge = jnp.where(lag == 0, last, ahead)
            for delta, (first, second) in parts.items():
                value = jnp.where(first, edge if delta else ahead, 0.0) + jnp.where(second, back, 0.0)
                sbuf[1 + delta, g, :, k * LANES:(k + 1) * LANES] = value.astype(jnp.bfloat16)

    sides = (row > 0).astype(jnp.int32) + (row < tiles - 1).astype(jnp.int32)
    pl.semaphore_wait(barrier, regions - 1 + sides * regions)

    for step, delta in links:
        to = peer(step, delta)
        copy = pltpu.make_async_remote_copy(
            src_ref=sbuf.at[1 + delta, to["ang"]], dst_ref=rbuf.at[me, slot(delta)],
            send_sem=send_sem.at[1 + delta], recv_sem=recv_sem.at[1 + delta],
            device_id=to, device_id_type=pl.DeviceIdType.MESH)
        when_there(delta, copy.start)
    weight_load.wait()
    rbuf[me, slot(0)] = sbuf[1, me]

    def group(delta):
        count = angles - 1 if delta == 0 else angles
        return pltpu.make_async_remote_copy(
            src_ref=sbuf.at[1 + delta, pl.ds(0, count)], dst_ref=rbuf.at[pl.ds(0, count), slot(delta)],
            send_sem=send_sem.at[1 + delta], recv_sem=recv_sem.at[1 + delta],
            device_id=peer(1, delta), device_id_type=pl.DeviceIdType.MESH)

    for delta in (0, -1, 1):
        when_there(-delta, group(delta).wait_recv)

    result = jnp.zeros((3 * rows, out.shape[1]), jnp.float32)
    for a in range(angles):
        w = jnp.concatenate([weights_v[a, k * cs:(k + 1) * cs] for k in range(shifts) for _ in range(rows)], axis=0)
        result = result + jnp.dot(rbuf[a], w, preferred_element_type=jnp.float32)
    out[...] = result[:rows] + result[rows:2 * rows] + result[2 * rows:]
    for delta in (0, -1, 1):
        when_there(delta, group(delta).wait_send)


def body(projections, flats, block_start, bp_weights):
    _, rows, width = projections.shape
    angles, cb, pixels = bp_weights.shape
    regions, tiles = lax.axis_size("ang"), lax.axis_size("row")
    cs = LANES // rows
    shifts = cb // cs
    table = jnp.asarray(filter_table(rows + 2 * HALO, width, cs), jnp.bfloat16)
    hbm = pl.BlockSpec(memory_space=pltpu.HBM)
    return pl.pallas_call(
        functools.partial(kernel, regions, tiles),
        name="fbp",
        out_shape=pltpu.VMEM((rows, pixels), jnp.float32),
        in_specs=[hbm, hbm, hbm, hbm, hbm],
        out_specs=pl.BlockSpec(memory_space=pltpu.VMEM),
        scratch_shapes=[
            pltpu.SMEM(block_start.shape, jnp.int32),
            pltpu.VMEM((rows, width), jnp.bfloat16),
            pltpu.VMEM((rows, width), jnp.float32),
            pltpu.VMEM(table.shape, jnp.bfloat16),
            pltpu.VMEM(bp_weights.shape, jnp.bfloat16),
            pltpu.VMEM((2 * width // LANES, rows, LANES), jnp.float32),
            pltpu.VMEM((regions * shifts * rows, width), jnp.bfloat16),
            pltpu.VMEM((3, regions, rows, shifts * LANES), jnp.bfloat16),
            pltpu.VMEM((angles, 3 * rows, shifts * LANES), jnp.bfloat16),
            pltpu.SemaphoreType.DMA((5,)),
            pltpu.SemaphoreType.DMA((3,)),
            pltpu.SemaphoreType.DMA((3,)),
        ],
        compiler_params=pltpu.CompilerParams(collective_id=0, has_side_effects=True, vmem_limit_bytes=65000000),
    )(block_start, projections, flats, table, bp_weights)


def solution(mesh):
    placed = (P(("scan", "ang"), "row", None), P(("scan", "row"), None), P(), P(None, None, "ang"))
    return jax.shard_map(
        body, mesh=mesh, in_specs=placed, out_specs=P(("scan", "row"), "ang"), check_vma=False
    )
```

time: 9.79 us -> 9.69 us (0.990)
  Pallas kernels: 9.03 us -> 8.93 us
where the time goes in v1:
time: 9.69 us; the launch traced here: 9.54 us
  Pallas kernels  8.93 us (92%)
  local copies, waits for them, and re-layouts  0.6 us (6%)
    pallas_call x1, Pallas kernels, body(): pl.pallas_call(functools.partial(kernel, regions, tiles), name='fbp', out...  8.93 us
    unnamed x1, local copies, waits for them, and re-layouts  0.6 us

profile of v1, /device:TPU:1, one launch (start us, length us, event | category | flops | bytes accessed | tf_op | source)
XLA Modules:
  0.0 9.5 jit_solution(15789409174389240204)
XLA Ops:
  0.0 8.9 %fbp.1 = f32[8,256]{1,0:T(8,128)S(1)} custom-call(s32[4,4]{1,0:T(4,128)} %starts.1, bf16[1,8,2560]{2,1,0:T(8,128)(2,1)} %proj.1, f32[8,2560]{1,0:T(8,128)} %flats.1, bf16[144,2560]{1,0:T(8,128)(2,1)} %constant.2.clone.table, bf16[4,32,256]{2,1,0:T(8,128)(2,1)} %weights.1), custom_call_target="tpu_custom_call" | custom-call | tf_op jit(solution)/shard_map/fbp/pallas_call | solution.py:166
  8.9 0.6 %copy.7 = f32[8,256]{1,0:T(8,128)} copy(f32[8,256]{1,0:T(8,128)S(1)} %fbp.1) | data formatting | bytes 16384

commit v2 on v1

--- a/solution.py
+++ b/solution.py
@@ -10,6 +10,9 @@
 
 HALO = 4
 LANES = 128
+FLAT_CUTS = 4
+PROJ_CUTS = 2
+CENTRE = 4
 paganin_beta = 8.0
 ramp_gain = 320.0
 
@@ -23,7 +26,8 @@
     taps = np.real(np.fft.ifft2(ramp[None, :] / (1.0 + paganin_beta * lam)))
     lags = tile_rows // 2 + 1
     place = (np.arange(columns)[:, None] - np.arange(width)[None, :]) % width
-    return taps[:lags][:, place].reshape(lags * columns, width)
+    sign = np.where(np.arange(width) < width // LANES // 2 * LANES, 1.0, -1.0)
+    return taps[:lags][:, place].reshape(lags * columns, width) * sign
 
 
 def kernel(regions, tiles, starts, proj, flats, table, weights, out,
@@ -49,12 +53,18 @@
         else:
             pl.when(row > 0 if delta < 0 else row < tiles - 1)(action)
 
-    loads = [pltpu.make_async_copy(proj.at[0], proj_v, load_sem.at[0]),
-             pltpu.make_async_copy(flats, flats_v, load_sem.at[1]),
+    loads = [pltpu.make_async_copy(flats, flats_v, load_sem.at[1]),
+             pltpu.make_async_copy(proj.at[0], proj_v, load_sem.at[0]),
              pltpu.make_async_copy(starts, starts_s, load_sem.at[3])]
     table_load = pltpu.make_async_copy(table, table_v, load_sem.at[4])
     weight_load = pltpu.make_async_copy(weights, weights_v, load_sem.at[2])
-    for copy in [*loads, table_load, weight_load]:
+    for n in range(FLAT_CUTS):
+        part = pl.ds(n * width // FLAT_CUTS, width // FLAT_CUTS)
+        pltpu.make_async_copy(flats.at[:, part], flats_v.at[:, part], load_sem.at[1]).start()
+    for n in range(PROJ_CUTS):
+        part = pl.ds(n * width // PROJ_CUTS, width // PROJ_CUTS)
+        pltpu.make_async_copy(proj.at[0, :, part], proj_v.at[:, part], load_sem.at[0]).start()
+    for copy in [loads[2], table_load, weight_load]:
         copy.start()
 
     barrier = pltpu.get_barrier_semaphore()
@@ -77,10 +87,10 @@
 
     pieces = [slice(b * LANES, (b + 1) * LANES) for b in range(blocks)]
     contrast = [1.0 - proj_v[:, p].astype(jnp.float32) / flats_v[:, p] for p in pieces]
-    mean = jnp.sum(sum(contrast), axis=1, keepdims=True) / width
+    centre = jnp.sum(sum(contrast[:CENTRE]), axis=1, keepdims=True) / (CENTRE * LANES)
     for b, x in enumerate(contrast):
-        xs[b] = x - mean
-        xs[b + blocks] = x - mean
+        xs[b] = x - centre
+        xs[b + blocks] = x - centre
 
     for g in range(regions):
         shifted = []
@@ -97,7 +107,10 @@
                 [y[b] for y in shifted], axis=0).astype(jnp.bfloat16)
 
     table_load.wait()
-    total = lax.dot_general(ys[...], table_v[...], (((1,), (1,)), ((), ())), preferred_element_type=jnp.float32)
+    cut = blocks // 2 * LANES
+    near, far = (lax.dot_general(ys[:, part], table_v[:, part], (((1,), (1,)), ((), ())), preferred_element_type=jnp.float32)
+                 for part in (slice(cut), slice(cut, width)))
+    total = near - far
     total = jnp.concatenate([total, jnp.zeros((total.shape[0], LANES - cs), jnp.float32)], axis=1)
 
     lag = lane // cs
@@ -130,29 +143,58 @@
         to = peer(step, delta)
         copy = pltpu.make_async_remote_copy(
             src_ref=sbuf.at[1 + delta, to["ang"]], dst_ref=rbuf.at[me, slot(delta)],
-            send_sem=send_sem.at[1 + delta], recv_sem=recv_sem.at[1 + delta],
+            send_sem=send_sem.at[1 + delta], recv_sem=recv_sem.at[me],
             device_id=to, device_id_type=pl.DeviceIdType.MESH)
         when_there(delta, copy.start)
     weight_load.wait()
     rbuf[me, slot(0)] = sbuf[1, me]
 
-    def group(delta):
-        count = angles - 1 if delta == 0 else angles
+    def sent(delta):
+        count = regions - 1 if delta == 0 else regions
         return pltpu.make_async_remote_copy(
             src_ref=sbuf.at[1 + delta, pl.ds(0, count)], dst_ref=rbuf.at[pl.ds(0, count), slot(delta)],
-            send_sem=send_sem.at[1 + delta], recv_sem=recv_sem.at[1 + delta],
+            send_sem=send_sem.at[1 + delta], recv_sem=recv_sem.at[me],
             device_id=peer(1, delta), device_id_type=pl.DeviceIdType.MESH)
 
+    inner = (row > 0) & (row < tiles - 1)
+    turn = jnp.where(me < regions // 2, 1, regions - 1)
+
+    def source(step):
+        return lax.rem(me + step * turn, regions)
+
+    def arrived(step):
+        angle = source(step)
+
+        def wait(count):
+            pltpu.make_async_remote_copy(
+                src_ref=rbuf.at[angle, pl.ds(0, count * rows)], dst_ref=rbuf.at[angle, pl.ds(0, count * rows)],
+                send_sem=send_sem.at[0], recv_sem=recv_sem.at[angle],
+                device_id=peer(1, 0), device_id_type=pl.DeviceIdType.MESH).wait_recv()
+
+        own = 1 if step == 0 else 0
+        pl.when(inner)(lambda: wait(3 - own))
+        pl.when(jnp.logical_not(inner))(lambda: wait(2 - own))
+
+    def projected(steps):
+        sums = []
+        for half_pixels in range(2):
+            pixels = pl.ds(half_pixels * (out.shape[1] // 2), out.shape[1] // 2)
+            result = 0.0
+            for step in steps:
+                angle = source(step)
+                w = jnp.concatenate(
+                    [weights_v[angle, k * cs:(k + 1) * cs, pixels] for k in range(shifts) for _ in range(rows)], axis=0)
+                result += jnp.dot(rbuf[angle], w, preferred_element_type=jnp.float32)
+            sums.append(result[:rows] + result[rows:2 * rows] + result[2 * rows:])
+        return jnp.concatenate(sums, axis=1)
+
+    for step in range(regions - 1):
+        arrived(step)
+    out[...] = projected(range(regions - 1))
+    arrived(regions - 1)
+    out[...] += projected([regions - 1])
     for delta in (0, -1, 1):
-        when_there(-delta, group(delta).wait_recv)
-
-    result = jnp.zeros((3 * rows, out.shape[1]), jnp.float32)
-    for a in range(angles):
-        w = jnp.concatenate([weights_v[a, k * cs:(k + 1) * cs] for k in range(shifts) for _ in range(rows)], axis=0)
-        result = result + jnp.dot(rbuf[a], w, preferred_element_type=jnp.float32)
-    out[...] = result[:rows] + result[rows:2 * rows] + result[2 * rows:]
-    for delta in (0, -1, 1):
-        when_there(delta, group(delta).wait_send)
+        when_there(delta, sent(delta).wait_send)
 
 
 def body(projections, flats, block_start, bp_weights):
@@ -181,7 +223,7 @@
             pltpu.VMEM((angles, 3 * rows, shifts * LANES), jnp.bfloat16),
             pltpu.SemaphoreType.DMA((5,)),
             pltpu.SemaphoreType.DMA((3,)),
-            pltpu.SemaphoreType.DMA((3,)),
+            pltpu.SemaphoreType.DMA((angles,)),
         ],
         compiler_params=pltpu.CompilerParams(collective_id=0, has_side_effects=True, vmem_limit_bytes=65000000),
     )(block_start, projections, flats, table, bp_weights)

time: 9.69 us -> 9.53 us (0.983)
  Pallas kernels: 8.93 us -> 8.78 us
    pallas_call x1, Pallas kernels: 8.93 us -> 8.78 us  [body(): pl.pallas_call(functools.partial(kernel, regions, tiles), name='fbp', out...]
where the time goes in v2:
time: 9.53 us; the launch traced here: 9.39 us
  Pallas kernels  8.78 us (92%)
  local copies, waits for them, and re-layouts  0.6 us (6%)
    pallas_call x1, Pallas kernels, body(): pl.pallas_call(functools.partial(kernel, regions, tiles), name='fbp', out...  8.78 us
    unnamed x1, local copies, waits for them, and re-layouts  0.6 us

profile of v2, /device:TPU:1, one launch (start us, length us, event | category | flops | bytes accessed | tf_op | source)
XLA Modules:
  0.0 9.4 jit_solution(12780220671205311103)
XLA Ops:
  0.0 8.8 %fbp.1 = f32[8,256]{1,0:T(8,128)S(1)} custom-call(s32[4,4]{1,0:T(4,128)} %starts.1, bf16[1,8,2560]{2,1,0:T(8,128)(2,1)} %proj.1, f32[8,2560]{1,0:T(8,128)} %flats.1, bf16[144,2560]{1,0:T(8,128)(2,1)} %constant.2.clone.table, bf16[4,32,256]{2,1,0:T(8,128)(2,1)} %weights.1), custom_call_target="tpu_custom_call" | custom-call | tf_op jit(solution)/shard_map/fbp/pallas_call | solution.py:208
  8.8 0.6 %copy.7 = f32[8,256]{1,0:T(8,128)} copy(f32[8,256]{1,0:T(8,128)S(1)} %fbp.1) | data formatting | bytes 16384

commit v3 on v2

--- a/solution.py
+++ b/solution.py
@@ -56,7 +56,8 @@
     loads = [pltpu.make_async_copy(flats, flats_v, load_sem.at[1]),
              pltpu.make_async_copy(proj.at[0], proj_v, load_sem.at[0]),
              pltpu.make_async_copy(starts, starts_s, load_sem.at[3])]
-    table_load = pltpu.make_async_copy(table, table_v, load_sem.at[4])
+    lags = rows + 1
+    table_load = pltpu.make_async_copy(table, table_v.at[pl.ds(0, lags * rows)], load_sem.at[4])
     weight_load = pltpu.make_async_copy(weights, weights_v, load_sem.at[2])
     for n in range(FLAT_CUTS):
         part = pl.ds(n * width // FLAT_CUTS, width // FLAT_CUTS)
@@ -64,8 +65,10 @@
     for n in range(PROJ_CUTS):
         part = pl.ds(n * width // PROJ_CUTS, width // PROJ_CUTS)
         pltpu.make_async_copy(proj.at[0, :, part], proj_v.at[:, part], load_sem.at[0]).start()
-    for copy in [loads[2], table_load, weight_load]:
-        copy.start()
+    loads[2].start()
+    for d in range(lags):
+        pltpu.make_async_copy(table.at[pl.ds(d * rows, rows)], table_v.at[pl.ds(d * cs, rows)], load_sem.at[4]).start()
+    weight_load.start()
 
     barrier = pltpu.get_barrier_semaphore()
     for step, delta in links:
@@ -92,6 +95,7 @@
         xs[b] = x - centre
         xs[b + blocks] = x - centre
 
+    table_load.wait()
     for g in range(regions):
         shifted = []
         for k in range(shifts):
@@ -106,8 +110,18 @@
             ys[g * shifts * rows:(g + 1) * shifts * rows, b * LANES:(b + 1) * LANES] = jnp.concatenate(
                 [y[b] for y in shifted], axis=0).astype(jnp.bfloat16)
 
-    table_load.wait()
-    cut = blocks // 2 * LANES
+    cut = blocks // 2
+    wide = lax.broadcasted_iota(jnp.int32, (2 * rows, LANES), 1)
+    for d in range(0, lags, 2):
+        pair = [e for e in (d, d + 1) if e < lags]
+        turned = [pltpu.roll(jnp.concatenate([table_v[e * cs:e * cs + rows, p] for e in pair], axis=0).astype(jnp.float32), rows, 1)
+                  for p in pieces]
+        for b, p in enumerate(pieces):
+            before = -turned[b - 1] if b in (0, cut) else turned[b - 1]
+            value = jnp.where(wide[:len(pair) * rows] < rows, before, turned[b]).astype(jnp.bfloat16)
+            for n, e in enumerate(pair):
+                table_v[e * cs + rows:(e + 1) * cs, p] = value[n * rows:(n + 1) * rows]
+    cut = cut * LANES
     near, far = (lax.dot_general(ys[:, part], table_v[:, part], (((1,), (1,)), ((), ())), preferred_element_type=jnp.float32)
                  for part in (slice(cut), slice(cut, width)))
     total = near - far
@@ -203,7 +217,8 @@
     regions, tiles = lax.axis_size("ang"), lax.axis_size("row")
     cs = LANES // rows
     shifts = cb // cs
-    table = jnp.asarray(filter_table(rows + 2 * HALO, width, cs), jnp.bfloat16)
+    table = jnp.asarray(filter_table(rows + 2 * HALO, width, rows), jnp.bfloat16)
+    lags = table.shape[0] // rows
     hbm = pl.BlockSpec(memory_space=pltpu.HBM)
     return pl.pallas_call(
         functools.partial(kernel, regions, tiles),
@@ -215,7 +230,7 @@
             pltpu.SMEM(block_start.shape, jnp.int32),
             pltpu.VMEM((rows, width), jnp.bfloat16),
             pltpu.VMEM((rows, width), jnp.float32),
-            pltpu.VMEM(table.shape, jnp.bfloat16),
+            pltpu.VMEM((lags * cs, width), jnp.bfloat16),
             pltpu.VMEM(bp_weights.shape, jnp.bfloat16),
             pltpu.VMEM((2 * width // LANES, rows, LANES), jnp.float32),
             pltpu.VMEM((regions * shifts * rows, width), jnp.bfloat16),

time: 9.53 us -> 9.46 us (level)
  Pallas kernels: 8.78 us -> 8.68 us
where the time goes in v3:
time: 9.46 us; the launch traced here: 9.29 us
  Pallas kernels  8.68 us (92%)
  local copies, waits for them, and re-layouts  0.6 us (6%)
    pallas_call x1, Pallas kernels, body(): pl.pallas_call(functools.partial(kernel, regions, tiles), name='fbp', out...  8.68 us
    unnamed x1, local copies, waits for them, and re-layouts  0.6 us

profile of v3, /device:TPU:1, one launch (start us, length us, event | category | flops | bytes accessed | tf_op | source)
XLA Modules:
  0.0 9.3 jit_solution(14873990959683658304)
XLA Ops:
  0.0 8.7 %fbp.1 = f32[8,256]{1,0:T(8,128)S(1)} custom-call(s32[4,4]{1,0:T(4,128)} %starts.1, bf16[1,8,2560]{2,1,0:T(8,128)(2,1)} %proj.1, f32[8,2560]{1,0:T(8,128)} %flats.1, bf16[72,2560]{1,0:T(8,128)(2,1)} %constant.2.clone.table, bf16[4,32,256]{2,1,0:T(8,128)(2,1)} %weights.1), custom_call_target="tpu_custom_call" | custom-call | tf_op jit(solution)/shard_map/fbp/pallas_call | solution.py:223
  8.7 0.6 %copy.7 = f32[8,256]{1,0:T(8,128)} copy(f32[8,256]{1,0:T(8,128)S(1)} %fbp.1) | data formatting | bytes 16384

commit v4 on v3

--- a/solution.py
+++ b/solution.py
@@ -10,8 +10,8 @@
 
 HALO = 4
 LANES = 128
-FLAT_CUTS = 4
-PROJ_CUTS = 2
+FLAT_CUTS = 2
+TABLE_CUTS = 2
 CENTRE = 4
 paganin_beta = 8.0
 ramp_gain = 320.0
@@ -62,12 +62,12 @@
     for n in range(FLAT_CUTS):
         part = pl.ds(n * width // FLAT_CUTS, width // FLAT_CUTS)
         pltpu.make_async_copy(flats.at[:, part], flats_v.at[:, part], load_sem.at[1]).start()
-    for n in range(PROJ_CUTS):
-        part = pl.ds(n * width // PROJ_CUTS, width // PROJ_CUTS)
-        pltpu.make_async_copy(proj.at[0, :, part], proj_v.at[:, part], load_sem.at[0]).start()
+    loads[1].start()
     loads[2].start()
     for d in range(lags):
-        pltpu.make_async_copy(table.at[pl.ds(d * rows, rows)], table_v.at[pl.ds(d * cs, rows)], load_sem.at[4]).start()
+        for n in range(TABLE_CUTS):
+            part = pl.ds(n * width // TABLE_CUTS, width // TABLE_CUTS)
+            pltpu.make_async_copy(table.at[pl.ds(d * rows, rows), part], table_v.at[pl.ds(d * cs, rows), part], load_sem.at[4]).start()
     weight_load.start()
 
     barrier = pltpu.get_barrier_semaphore()
@@ -148,27 +148,22 @@
             edge = jnp.where(lag == 0, last, ahead)
             for delta, (first, second) in parts.items():
                 value = jnp.where(first, edge if delta else ahead, 0.0) + jnp.where(second, back, 0.0)
-                sbuf[1 + delta, g, :, k * LANES:(k + 1) * LANES] = value.astype(jnp.bfloat16)
+                sbuf[(1 + delta) * regions + g, :, k * LANES:(k + 1) * LANES] = value.astype(jnp.bfloat16)
 
     sides = (row > 0).astype(jnp.int32) + (row < tiles - 1).astype(jnp.int32)
     pl.semaphore_wait(barrier, regions - 1 + sides * regions)
 
     for step, delta in links:
         to = peer(step, delta)
+        low = (to["ang"] < regions // 2).astype(jnp.int32)
+        final = (low if step == 1 else 0) + (1 - low if step == regions - 1 else 0)
         copy = pltpu.make_async_remote_copy(
-            src_ref=sbuf.at[1 + delta, to["ang"]], dst_ref=rbuf.at[me, slot(delta)],
-            send_sem=send_sem.at[1 + delta], recv_sem=recv_sem.at[me],
+            src_ref=sbuf.at[(1 + delta) * regions + to["ang"]], dst_ref=rbuf.at[me, slot(delta)],
+            send_sem=send_sem, recv_sem=recv_sem.at[final],
             device_id=to, device_id_type=pl.DeviceIdType.MESH)
         when_there(delta, copy.start)
     weight_load.wait()
-    rbuf[me, slot(0)] = sbuf[1, me]
-
-    def sent(delta):
-        count = regions - 1 if delta == 0 else regions
-        return pltpu.make_async_remote_copy(
-            src_ref=sbuf.at[1 + delta, pl.ds(0, count)], dst_ref=rbuf.at[pl.ds(0, count), slot(delta)],
-            send_sem=send_sem.at[1 + delta], recv_sem=recv_sem.at[me],
-            device_id=peer(1, delta), device_id_type=pl.DeviceIdType.MESH)
+    rbuf[me, slot(0)] = sbuf[regions + me]
 
     inner = (row > 0) & (row < tiles - 1)
     turn = jnp.where(me < regions // 2, 1, regions - 1)
@@ -176,18 +171,15 @@
     def source(step):
         return lax.rem(me + step * turn, regions)
 
-    def arrived(step):
-        angle = source(step)
-
+    def settled(full, short, sem, kind):
         def wait(count):
-            pltpu.make_async_remote_copy(
-                src_ref=rbuf.at[angle, pl.ds(0, count * rows)], dst_ref=rbuf.at[angle, pl.ds(0, count * rows)],
-                send_sem=send_sem.at[0], recv_sem=recv_sem.at[angle],
-                device_id=peer(1, 0), device_id_type=pl.DeviceIdType.MESH).wait_recv()
-
-        own = 1 if step == 0 else 0
-        pl.when(inner)(lambda: wait(3 - own))
-        pl.when(jnp.logical_not(inner))(lambda: wait(2 - own))
+            units = sbuf.at[pl.ds(0, count)]
+            kind(pltpu.make_async_remote_copy(
+                src_ref=units, dst_ref=units, send_sem=send_sem, recv_sem=recv_sem.at[sem],
+                device_id=peer(1, 0), device_id_type=pl.DeviceIdType.MESH))
+
+        pl.when(inner)(lambda: wait(full))
+        pl.when(jnp.logical_not(inner))(lambda: wait(short))
 
     def projected(steps):
         sums = []
@@ -202,13 +194,11 @@
             sums.append(result[:rows] + result[rows:2 * rows] + result[2 * rows:])
         return jnp.concatenate(sums, axis=1)
 
-    for step in range(regions - 1):
-        arrived(step)
+    settled(3 * regions - 4, 2 * regions - 3, 0, lambda copy: copy.wait_recv())
     out[...] = projected(range(regions - 1))
-    arrived(regions - 1)
+    settled(3, 2, 1, lambda copy: copy.wait_recv())
     out[...] += projected([regions - 1])
-    for delta in (0, -1, 1):
-        when_there(delta, sent(delta).wait_send)
+    settled(3 * regions - 1, 2 * regions - 1, 0, lambda copy: copy.wait_send())
 
 
 def body(projections, flats, block_start, bp_weights):
@@ -234,11 +224,11 @@
             pltpu.VMEM(bp_weights.shape, jnp.bfloat16),
             pltpu.VMEM((2 * width // LANES, rows, LANES), jnp.float32),
             pltpu.VMEM((regions * shifts * rows, width), jnp.bfloat16),
-            pltpu.VMEM((3, regions, rows, shifts * LANES), jnp.bfloat16),
+            pltpu.VMEM((3 * regions, rows, shifts * LANES), jnp.bfloat16),
             pltpu.VMEM((angles, 3 * rows, shifts * LANES), jnp.bfloat16),
             pltpu.SemaphoreType.DMA((5,)),
-            pltpu.SemaphoreType.DMA((3,)),
-            pltpu.SemaphoreType.DMA((angles,)),
+            pltpu.SemaphoreType.DMA,
+            pltpu.SemaphoreType.DMA((2,)),
         ],
         compiler_params=pltpu.CompilerParams(collective_id=0, has_side_effects=True, vmem_limit_bytes=65000000),
     )(block_start, projections, flats, table, bp_weights)

time: 9.46 us -> 9.34 us (0.987)
  Pallas kernels: 8.68 us -> 8.57 us
    pallas_call x1, Pallas kernels: 8.68 us -> 8.57 us  [body(): pl.pallas_call(functools.partial(kernel, regions, tiles), name='fbp', out...]
where the time goes in v4:
time: 9.34 us; the launch traced here: 9.18 us
  Pallas kernels  8.57 us (92%)
  local copies, waits for them, and re-layouts  0.6 us (6%)
    pallas_call x1, Pallas kernels, body(): pl.pallas_call(functools.partial(kernel, regions, tiles), name='fbp', out...  8.57 us
    unnamed x1, local copies, waits for them, and re-layouts  0.6 us

profile of v4, /device:TPU:1, one launch (start us, length us, event | category | flops | bytes accessed | tf_op | source)
XLA Modules:
  0.0 9.2 jit_solution(13687246800828550075)
XLA Ops:
  0.0 8.6 %fbp.1 = f32[8,256]{1,0:T(8,128)S(1)} custom-call(s32[4,4]{1,0:T(4,128)} %starts.1, bf16[1,8,2560]{2,1,0:T(8,128)(2,1)} %proj.1, f32[8,2560]{1,0:T(8,128)} %flats.1, bf16[72,2560]{1,0:T(8,128)(2,1)} %constant.2.clone.table, bf16[4,32,256]{2,1,0:T(8,128)(2,1)} %weights.1), custom_call_target="tpu_custom_call" | custom-call | tf_op jit(solution)/shard_map/fbp/pallas_call | solution.py:213
  8.6 0.6 %copy.7 = f32[8,256]{1,0:T(8,128)} copy(f32[8,256]{1,0:T(8,128)S(1)} %fbp.1) | data formatting | bytes 16384

commit v5 on v4

v5 whole, which is shorter than its diff:
```python
import functools

import jax
import jax.numpy as jnp
import numpy as np
from jax import lax
from jax.experimental import pallas as pl
from jax.experimental.pallas import tpu as pltpu
from jax.sharding import PartitionSpec as P

HALO = 4
LANES = 128
FLAT_CUTS = 2
TABLE_CUTS = 2
CENTRE = 4
paganin_beta = 8.0
ramp_gain = 320.0


def filter_table(tile_rows, width, columns):
    u = np.arange(tile_rows, dtype=np.float64)
    v = np.arange(width, dtype=np.float64)
    lam = (4.0 * np.sin(np.pi * u / tile_rows) ** 2)[:, None] + (4.0 * np.sin(np.pi * v / width) ** 2)[None, :]
    folded = np.minimum(v, width - v)
    ramp = ramp_gain * (folded / width) * (0.5 + 0.5 * np.cos(2.0 * np.pi * folded / width))
    taps = np.real(np.fft.ifft2(ramp[None, :] / (1.0 + paganin_beta * lam)))
    lags = tile_rows // 2 + 1
    place = (np.arange(columns)[:, None] - np.arange(width)[None, :]) % width
    sign = np.where(np.arange(width) < width // LANES // 2 * LANES, 1.0, -1.0)
    return taps[:lags][:, place].reshape(lags * columns, width) * sign


def kernel(regions, tiles, starts, proj, flats, table, weights, out,
           starts_s, proj_v, flats_v, table_v, weights_v, xs, ys, sbuf, rbuf,
           load_sem, send_sem, recv_sem):
    rows, width = flats.shape
    blocks = width // LANES
    angles, cb, _ = weights.shape
    half = rows // 2
    cs = LANES // (2 * rows)
    shifts = cb // cs
    pairs = shifts // 2
    lags = rows + 1
    order = [(0, 0), (1, 0), *[(0, d) for d in range(1, rows)], (1, rows - 1), *[(1, d) for d in range(1, rows - 1)]]
    me = lax.axis_index("ang")
    row = lax.axis_index("row")

    def peer(step, delta):
        return {"ang": lax.rem(me + step, regions), "row": lax.rem(row + delta + tiles, tiles)}

    links = [(step, delta) for step in (*range(1, regions), 0) for delta in (-1, 1, 0) if (step, delta) != (0, 0)]

    def when_there(delta, action):
        if delta == 0:
            action()
        else:
            pl.when(row > 0 if delta < 0 else row < tiles - 1)(action)

    loads = [pltpu.make_async_copy(flats, flats_v, load_sem.at[1]),
             pltpu.make_async_copy(proj.at[0], proj_v, load_sem.at[0]),
             pltpu.make_async_copy(starts, starts_s, load_sem.at[3])]
    table_load = pltpu.make_async_copy(table, table_v, load_sem.at[4])
    weight_load = pltpu.make_async_copy(weights, weights_v, load_sem.at[2])
    for n in range(FLAT_CUTS):
        part = pl.ds(n * width // FLAT_CUTS, width // FLAT_CUTS)
        pltpu.make_async_copy(flats.at[:, part], flats_v.at[:, part], load_sem.at[1]).start()
    loads[1].start()
    loads[2].start()
    for d in range(lags):
        for n in range(TABLE_CUTS):
            part = pl.ds(n * width // TABLE_CUTS, width // TABLE_CUTS)
            pltpu.make_async_copy(table.at[pl.ds(d * cs, cs), part], table_v.at[pl.ds(d * cs, cs), part], load_sem.at[4]).start()
    weight_load.start()

    barrier = pltpu.get_barrier_semaphore()
    for step, delta in links:
        when_there(delta, lambda: pl.semaphore_signal(
            barrier, inc=1, device_id=peer(step, delta), device_id_type=pl.DeviceIdType.MESH))

    def slot(delta):
        return pl.ds((1 + delta) * rows, rows)

    zeros = jnp.zeros((angles, rows, pairs * LANES), jnp.bfloat16)
    pl.when(row == tiles - 1)(lambda: rbuf.at[:, slot(-1)].__setitem__(..., zeros))
    pl.when(row == 0)(lambda: rbuf.at[:, slot(1)].__setitem__(..., zeros))

    lane = lax.broadcasted_iota(jnp.int32, (rows, LANES), 1)
    sub = lax.broadcasted_iota(jnp.int32, (rows, LANES), 0)

    for copy in loads:
        copy.wait()

    pieces = [slice(b * LANES, (b + 1) * LANES) for b in range(blocks)]
    contrast = [1.0 - proj_v[:, p].astype(jnp.float32) / flats_v[:, p] for p in pieces]
    centre = jnp.sum(sum(contrast[:CENTRE]), axis=1, keepdims=True) / (CENTRE * LANES)
    for b, x in enumerate(contrast):
        xs[b] = x - centre
        xs[b + blocks] = x - centre

    spot = lane // cs
    lag = jnp.where(spot < 2, 0, jnp.where(spot < rows, spot - 1, jnp.where(spot < rows + 2, rows - 1, spot - rows - 1)))
    odd = (spot == 1) | (spot > rows)
    up, down = lax.rem(sub + rows - lag, rows), lax.rem(sub + lag, rows)
    inside = [sub >= lag, (lag > 0) & (sub + lag < rows)]
    wrapped = [(sub < lag) | (lag == 0), sub + lag >= rows]
    parts = {-1: [wrapped[0] & (up < half), wrapped[1] & (down < half)],
             1: [wrapped[0] & (up >= half), wrapped[1] & (down >= half)],
             0: inside}
    bits = [1 << n for n in range((rows - 1).bit_length())]
    def filtered(group):
        deep = shifts * rows
        for region in group:
            shifted = []
            for k in range(shifts):
                start = starts_s[me, region] + k * cs
                first = start // LANES
                rest = lax.rem(start, LANES)
                shift = lax.rem(LANES - rest, LANES)
                low = lane < LANES - rest
                turned = [pltpu.roll(xs[first + b], shift, 1) for b in range(blocks + 1)]
                shifted.append([jnp.where(low, turned[b], turned[b + 1]) for b in range(blocks)])
            for b in range(blocks):
                place = region * deep
                ys[place:place + deep, pieces[b]] = jnp.concatenate(
                    [y[b] for y in shifted], axis=0).astype(jnp.bfloat16)
        cut = blocks // 2 * LANES
        begin = group[0] * deep
        end = begin + len(group) * deep
        near, far = (lax.dot_general(
            ys[begin:end, part], jnp.concatenate([table_v[d * cs:(d + 1) * cs, part] for _, d in [*order, (0, rows), (1, rows)]], axis=0),
            (((1,), (1,)), ((), ())), preferred_element_type=jnp.float32) for part in (slice(cut), slice(cut, width)))
        total = near - far
        total = jnp.concatenate([total, jnp.zeros((total.shape[0], LANES - 2 * cs), jnp.float32)], axis=1)
        for n, region in enumerate(group):
            for k in range(pairs):
                base = n * deep + k * 2 * rows
                even_rows, odd_rows = total[base:base + rows], total[base + rows:base + 2 * rows]
                tile = jnp.where(odd, odd_rows[:, :LANES], even_rows[:, :LANES])
                last = jnp.where(odd, odd_rows[:, LANES:], even_rows[:, LANES:])
                ahead, back = tile, tile
                for bit in bits:
                    turn = (lag & bit) > 0
                    ahead = jnp.where(turn, pltpu.roll(ahead, bit, 0), ahead)
                    back = jnp.where(turn, pltpu.roll(back, rows - bit, 0), back)
                edge = jnp.where(lag == 0, last, ahead)
                for delta, (first, second) in parts.items():
                    value = jnp.where(first, edge if delta else ahead, 0.0) + jnp.where(second, back, 0.0)
                    sbuf[(1 + delta) * regions + region, :, k * LANES:(k + 1) * LANES] = value.astype(jnp.bfloat16)

    def send(group):
        for region in group:
            last = (region + (regions - 1 if region < regions // 2 else 1)) % regions
            final = (me == last).astype(jnp.int32)
            for delta in (-1, 1, 0):
                copy = pltpu.make_async_remote_copy(
                    src_ref=sbuf.at[(1 + delta) * regions + region], dst_ref=rbuf.at[me, slot(delta)],
                    send_sem=send_sem, recv_sem=recv_sem.at[final],
                    device_id={"ang": region, "row": lax.rem(row + delta + tiles, tiles)},
                    device_id_type=pl.DeviceIdType.MESH)
                if delta == 0:
                    pl.when(me != region)(copy.start)
                else:
                    when_there(delta, copy.start)

    table_load.wait()
    filtered([0])
    sides = (row > 0).astype(jnp.int32) + (row < tiles - 1).astype(jnp.int32)
    pl.semaphore_wait(barrier, regions - 1 + sides * regions)
    send([0])
    filtered([*range(1, regions)])
    send([*range(1, regions)])
    weight_load.wait()
    rbuf[me, slot(0)] = sbuf[regions + me]

    inner = (row > 0) & (row < tiles - 1)
    turn = jnp.where(me < regions // 2, 1, regions - 1)

    def source(step):
        return lax.rem(me + step * turn, regions)

    def settled(full, short, sem, kind):
        def wait(count):
            units = sbuf.at[pl.ds(0, count)]
            kind(pltpu.make_async_remote_copy(
                src_ref=units, dst_ref=units, send_sem=send_sem, recv_sem=recv_sem.at[sem],
                device_id=peer(1, 0), device_id_type=pl.DeviceIdType.MESH))

        pl.when(inner)(lambda: wait(full))
        pl.when(jnp.logical_not(inner))(lambda: wait(short))

    def projected(steps):
        sums = []
        for half_pixels in range(2):
            pixels = pl.ds(half_pixels * (out.shape[1] // 2), out.shape[1] // 2)
            result = 0.0
            for step in steps:
                angle = source(step)
                w = jnp.concatenate(
                    [weights_v[angle, (2 * k + side) * cs:(2 * k + side + 1) * cs, pixels]
                     for k in range(pairs) for side, _ in order], axis=0)
                result += jnp.dot(rbuf[angle], w, preferred_element_type=jnp.float32)
            sums.append(result[:rows] + result[rows:2 * rows] + result[2 * rows:])
        return jnp.concatenate(sums, axis=1)

    settled(3 * regions - 4, 2 * regions - 3, 0, lambda copy: copy.wait_recv())
    out[...] = projected(range(regions - 1))
    settled(3, 2, 1, lambda copy: copy.wait_recv())
    out[...] += projected([regions - 1])
    settled(3 * regions - 1, 2 * regions - 1, 0, lambda copy: copy.wait_send())


def body(projections, flats, block_start, bp_weights):
    _, rows, width = projections.shape
    angles, cb, pixels = bp_weights.shape
    regions, tiles = lax.axis_size("ang"), lax.axis_size("row")
    cs = LANES // (2 * rows)
    pairs = cb // cs // 2
    table = jnp.asarray(filter_table(rows + 2 * HALO, width, cs), jnp.bfloat16)
    hbm = pl.BlockSpec(memory_space=pltpu.HBM)
    return pl.pallas_call(
        functools.partial(kernel, regions, tiles),
        name="fbp",
        out_shape=pltpu.VMEM((rows, pixels), jnp.float32),
        in_specs=[hbm, hbm, hbm, hbm, hbm],
        out_specs=pl.BlockSpec(memory_space=pltpu.VMEM),
        scratch_shapes=[
            pltpu.SMEM(block_start.shape, jnp.int32),
            pltpu.VMEM((rows, width), jnp.bfloat16),
            pltpu.VMEM((rows, width), jnp.float32),
            pltpu.VMEM(table.shape, jnp.bfloat16),
            pltpu.VMEM(bp_weights.shape, jnp.bfloat16),
            pltpu.VMEM((2 * width // LANES, rows, LANES), jnp.float32),
            pltpu.VMEM((regions * (cb // cs) * rows, width), jnp.bfloat16),
            pltpu.VMEM((3 * regions, rows, pairs * LANES), jnp.bfloat16),
            pltpu.VMEM((angles, 3 * rows, pairs * LANES), jnp.bfloat16),
            pltpu.SemaphoreType.DMA((5,)),
            pltpu.SemaphoreType.DMA,
            pltpu.SemaphoreType.DMA((2,)),
        ],
        compiler_params=pltpu.CompilerParams(collective_id=0, has_side_effects=True, vmem_limit_bytes=65000000),
    )(block_start, projections, flats, table, bp_weights)


def solution(mesh):
    placed = (P(("scan", "ang"), "row", None), P(("scan", "row"), None), P(), P(None, None, "ang"))
    return jax.shard_map(
        body, mesh=mesh, in_specs=placed, out_specs=P(("scan", "row"), "ang"), check_vma=False
    )
```

time: 9.34 us -> 9.27 us (level)
  no operation moved by 1% of the time
where the time goes in v5:
time: 9.27 us; the launch traced here: 9.11 us
  Pallas kernels  8.5 us (92%)
  local copies, waits for them, and re-layouts  0.6 us (6%)
    pallas_call x1, Pallas kernels, body(): pl.pallas_call(functools.partial(kernel, regions, tiles), name='fbp', out...  8.5 us
    unnamed x1, local copies, waits for them, and re-layouts  0.6 us

profile of v5, /device:TPU:1, one launch (start us, length us, event | category | flops | bytes accessed | tf_op | source)
XLA Modules:
  0.0 9.1 jit_solution(17061488324862295559)
XLA Ops:
  0.0 8.5 %fbp.1 = f32[8,256]{1,0:T(8,128)S(1)} custom-call(s32[4,4]{1,0:T(4,128)} %starts.1, bf16[1,8,2560]{2,1,0:T(8,128)(2,1)} %proj.1, f32[8,2560]{1,0:T(8,128)} %flats.1, bf16[72,2560]{1,0:T(8,128)(2,1)} %constant.2.clone.table, bf16[4,32,256]{2,1,0:T(8,128)(2,1)} %weights.1), custom_call_target="tpu_custom_call" | custom-call | tf_op jit(solution)/shard_map/fbp/pallas_call | solution.py:220
  8.5 0.6 %copy.7 = f32[8,256]{1,0:T(8,128)} copy(f32[8,256]{1,0:T(8,128)S(1)} %fbp.1) | data formatting | bytes 16384
